TPU v7x, 256 devices: a whole 4x4x8 slice. The times are simulated.
256 devices in a mesh: wide: 64 (over z, y, core), narrow: 4 (over x).
Axes of the slice: x: 4, y: 4, z: 8, core: 2. Of those that a mesh axis runs over, the one named last changes fastest.
Arguments:
- coords_inner: float32 [2, 65536], P(None, ('wide', 'narrow')), may hold values from -1 to 1
- velocity: float32 [2, 65536], P(None, ('wide', 'narrow')), may hold values from -6 to 6
- source: float32 [65536], P(('wide', 'narrow')), may hold values from -6 to 6
- coords_edge: float32 [2, 32768], P(None, ('wide', 'narrow')), may hold values from -1 to 1
- flux_weight: float32 [2, 32768], P(None, ('wide', 'narrow')), may hold values from -6 to 6
- owner: int32 [32768, 1], P(('wide', 'narrow')), may hold values from 0 to 63; in each aligned block of 128 rows (0 to 127, 128 to 255, ...) at most 4 rows name the same one
- local_face: int32 [32768], P(('wide', 'narrow')), may hold values from 0 to 127
- w_first: float32 [2, 512], replicated, may hold values from -4 to 4
- b_first: float32 [512], replicated, may hold values from -3 to 3
- w_hidden: float32 [4, 512, 512], replicated, may hold values from -0.25 to 0.25
- b_hidden: float32 [4, 512], replicated, may hold values from -3 to 3
- w_last: float32 [512], replicated, may hold values from -0.25 to 0.25
Outputs:
- face_integral: float32 [8192], P('wide')
- grad_first: float32 [2, 512], replicated
- grad_hidden: float32 [4, 512, 512], replicated
- grad_last: float32 [512], replicated
Inputs may be any that keep to these rules, and one draw needn't show every extreme that they name: Among the 128 face points of one device no owner appears more than 4 times, and some owner appears exactly 4 times.
All inputs are finite; a program needn't handle non-finite values.
Results may differ from a plain program's by a relative error of at most 0.0003.
Values sent between devices are 32-bit elements; how exact they have to be, the bound alone decides.
A program may use at most 128 MiB of HBM per device.

v0:
```python
import math
import jax
import jax.numpy as jnp
from jax import lax
from jax.sharding import PartitionSpec as P

FACE_DEV = 128
penalty_weight = 4.0
BOTH = ("wide", "narrow")
precise = lax.Precision.HIGH


def forward(coords, direction, w_first, b_first, w_hidden, b_hidden, w_last):
    hidden = jnp.tanh(
        coords[0][:, None] * w_first[0][None] + coords[1][:, None] * w_first[1][None] + b_first
    )
    tangent = (1.0 - hidden * hidden) * (
        direction[0][:, None] * w_first[0][None] + direction[1][:, None] * w_first[1][None]
    )
    points = hidden.shape[0]
    kept = [(hidden, None, tangent)]
    for level in range(w_hidden.shape[0]):
        product = jnp.dot(jnp.concatenate([hidden, tangent], 0), w_hidden[level], precision=precise)
        hidden = jnp.tanh(product[:points] + b_hidden[level])
        slope = product[points:]
        tangent = (1.0 - hidden * hidden) * slope
        kept.append((hidden, slope, tangent))
    value = jnp.sum(hidden * w_last[None], 1)
    slopes = jnp.sum(tangent * w_last[None], 1)
    return (value, slopes, kept)


def backward(coords, direction, kept, hidden_cot, tangent_cot, w_first, w_hidden):
    grads = []
    for level in reversed(range(w_hidden.shape[0])):
        hidden, slope, _ = kept[level + 1]
        gate = 1.0 - hidden * hidden
        product_cot = gate * tangent_cot
        sum_cot = gate * (hidden_cot - 2.0 * hidden * slope * tangent_cot)
        cots = jnp.concatenate([sum_cot, product_cot], 0)
        below = jnp.concatenate([kept[level][0], kept[level][2]], 0)
        grads.append(lax.dot_general(below, cots, (((0,), (0,)), ((), ())), precision=precise))
        down = lax.dot_general(cots, w_hidden[level], (((1,), (1,)), ((), ())), precision=precise)
        points = hidden.shape[0]
        hidden_cot, tangent_cot = (down[:points], down[points:])
    hidden, _, _ = kept[0]
    gate = 1.0 - hidden * hidden
    start = direction[0][:, None] * w_first[0][None] + direction[1][:, None] * w_first[1][None]
    start_cot = gate * tangent_cot
    sum_cot = gate * (hidden_cot - 2.0 * hidden * start * tangent_cot)
    first = jnp.stack(
        [
            jnp.sum(coords[j][:, None] * sum_cot + direction[j][:, None] * start_cot, 0)
            for j in range(2)
        ]
    )
    return (first, jnp.stack(grads[::-1], 0))


def local(
    coords_inner,
    velocity,
    source,
    coords_edge,
    flux_weight,
    owner,
    local_face,
    w_first,
    b_first,
    w_hidden,
    b_hidden,
    w_last,
):
    devices = lax.axis_size(BOTH)
    inner_rows = coords_inner.shape[1]
    edge_rows = coords_edge.shape[1]
    inner_scale = 2.0 / math.sqrt(inner_rows * devices)
    face_scale = 2.0 * penalty_weight / math.sqrt(FACE_DEV * lax.axis_size("wide"))
    net = (w_first, b_first, w_hidden, b_hidden, w_last)
    _, flux, kept_edge = forward(coords_edge, flux_weight, *net)
    face = owner[:, 0] * FACE_DEV + local_face
    mine = jnp.stack([flux, face.astype(jnp.float32)], 0)
    everyone = lax.all_gather(mine, BOTH)
    all_flux = everyone[:, 0].reshape(-1)
    all_face = everyone[:, 1].reshape(-1)

    def sums(wanted):
        return jnp.sum(
            jnp.where(wanted.astype(jnp.float32)[:, None] == all_face[None], all_flux[None], 0.0), 1
        )

    reached = sums(face)
    integral = sums(lax.axis_index("wide") * FACE_DEV + jnp.arange(FACE_DEV))
    value, slopes, kept_inner = forward(coords_inner, velocity, *net)
    inner_cot = inner_scale * (slopes + value - source)
    edge_cot = face_scale * reached
    coords = jnp.concatenate([coords_inner, coords_edge], 1)
    direction = jnp.concatenate([velocity, flux_weight], 1)
    kept = [
        tuple((None if a is None else jnp.concatenate([a, b], 0) for a, b in zip(one, two)))
        for one, two in zip(kept_inner, kept_edge)
    ]
    hidden_out = jnp.concatenate([inner_cot, jnp.zeros_like(edge_cot)])[:, None]
    tangent_out = jnp.concatenate([inner_cot, edge_cot])[:, None]
    last = jnp.sum(hidden_out * kept[-1][0] + tangent_out * kept[-1][2], 0)
    first, hidden = backward(
        coords,
        direction,
        kept,
        hidden_out * w_last[None],
        tangent_out * w_last[None],
        w_first,
        w_hidden,
    )
    first, hidden, last = lax.psum((first, hidden, last), BOTH)
    return (integral, first, hidden, last)


def solution(mesh):
    points = P(None, BOTH)
    in_specs = (
        points,
        points,
        P(BOTH),
        points,
        points,
        P(BOTH, None),
        P(BOTH),
        P(),
        P(),
        P(),
        P(),
        P(),
    )
    out_specs = (P("wide"), P(), P(), P())
    return jax.shard_map(local, mesh=mesh, in_specs=in_specs, out_specs=out_specs, check_vma=False)
```

profile of v0, /device:TPU:2, one launch (start us, length us, event | category | flops | bytes accessed | tf_op | source)
XLA Modules:
  0.0 388.6 jit_solution(4115349576246029402)
XLA Ops:
  7.2 0.0 all-reduce.4.cloned.1.call-start
  7.2 0.8 fusion.155
  8.0 0.8 fusion.156
  8.7 0.8 fusion.154
  9.5 0.9 fusion.153
  10.4 0.8 slice_bitcast_fusion.1
  11.1 0.8 add_tanh_fusion.1
  12.0 1.8 fusion.78
  13.8 0.0 copy-start
  13.8 0.1 subtract_multiply_fusion.7
  13.9 2.0 fusion.74
  15.9 0.1 subtract_multiply_fusion.6
  16.0 0.3 copy-done
  16.3 0.7 fusion.70
  17.0 0.0 copy-start.8
  17.0 0.0 copy-start.9
  17.0 0.0 copy-start.1
  17.0 0.1 subtract_multiply_fusion.5
  17.1 0.6 fusion.66
  17.8 0.0 copy-done.8
  17.8 0.0 copy-done.9
  17.8 0.0 copy-start.2
  17.8 0.0 copy-done.1
  17.8 0.2 multiply_reduce_fusion.2
  18.0 67.6 %all-gather.1 = f32[256,2,128]{2,1,0:T(2,128)S(1)} all-gather(f32[1,2,128]{2,1,0:T(2,128)S(1)} %maximum_bitcast_fusion), channel_id=2, replica_groups=mesh['wide'=64,'narrow'=4] {'wide','narrow'}, dimensions={0}, use_global_device_ids=true | all-gather | bytes 263168 | tf_op jit(solution)/shard_map/all_gather | solution.py:83
  85.6 0.2 fusion.152
  85.8 4.7 %select_reduce_fusion = (f32[128]{0:T(128)S(1)}, f32[128]{0:T(128)}) fusion(f32[32768]{0:T(1024)S(1)} %bitcast.67, f32[32768]{0:T(1024)S(1)} %bitcast.66, f32[128]{0:T(128)S(1)} %get-tuple-element.74, f32[128]{0:T(128)S(1)} %get-tuple-element.75), kind=kLoop, calls=%fused_computation | loop fusion | flops 25165568 | bytes 264192 | tf_op jit(solution)/shard_map/reduce_sum | solution.py:88
  90.5 0.0 copy-done.2
  90.5 0.3 add_tanh_fusion
  90.8 1.0 fusion.48
  91.8 0.2 subtract_multiply_fusion.3
  92.0 1.1 fusion.52
  93.0 0.2 subtract_multiply_fusion.2
  93.2 1.0 fusion.56
  94.3 0.2 subtract_multiply_fusion.1
  94.5 1.1 fusion.60
  95.5 0.0 copy-start.7
  95.5 0.2 multiply_reduce_fusion
  95.8 0.4 copy-done.7
  96.2 0.4 fusion.102
  96.6 1.5 fusion.32
  98.2 1.7 fusion.47
  99.9 0.4 fusion.97
  100.3 1.5 fusion.35
  101.8 1.5 fusion.46
  103.3 0.4 fusion.96
  103.7 1.5 fusion.38
  105.2 1.5 fusion.45
  106.6 0.4 fusion.95
  107.0 1.5 fusion.41
  108.5 2.5 pad_maximum_fusion
  111.0 0.0 copy-start.3
  111.0 0.0 copy-start.5
  111.0 0.0 copy-start.4
  111.0 0.0 all-reduce.4.cloned.1.call-update
  111.0 0.6 copy-done.3
  111.7 0.0 copy-done.5
  111.7 0.0 copy-done.4
  111.7 0.0 copy-done.6
  111.7 2.7 fusion.44
  114.4 0.6 add_reduce_fusion.1
  115.0 73.2 %all-reduce.1 = (f32[2,512]{1,0:T(2,128)}, f32[512]{0:T(512)}) all-reduce(f32[2,512]{1,0:T(2,128)S(1)} %pad_maximum_fusion.18, f32[512]{0:T(512)S(1)} %get-tuple-element.43), channel_id=1, replica_groups=mesh['wide'=64,'narrow'=4] {'wide','narrow'}, use_global_device_ids=true, to_apply=%region_7.8 | all-reduce | flops 1536 | bytes 12288 | tf_op jit(solution)/shard_map/psum | solution.py:115
  188.3 188.8 %all-reduce.4.cloned.1.call-done = f32[4,512,512]{2,1,0:T(8,128)} async-done(((f32[4,512,512]{2,1,0:T(8,128)}), f32[4,512,512]{2,1,0:T(8,128)}) %all-reduce.4.cloned.1.call-update) | async-done | bytes 4194320 | tf_op jit(solution)/shard_map/psum | solution.py:115
  377.1 4.6 %copy.19 = f32[4,512,512]{2,1,0:T(8,128)} copy(f32[4,512,512]{2,1,0:T(8,128)} %all-reduce.4.cloned.1.call-done) | data formatting | bytes 8388608
  (12 shorter events, 0.1 us)
Async XLA Ops:
  7.2 369.9 %all-reduce.4.cloned.1.call-start = ((), (), s32[]{:S(2)}) async-start(), calls=%async_computation | async-start | bytes 8388608 | tf_op jit(solution)/shard_map/psum | solution.py:115
  13.8 2.5 copy-start
  17.0 0.8 copy-start.8
  17.0 0.8 copy-start.9
  17.0 0.8 copy-start.1
  17.8 72.7 %copy-start.2 = (f32[512]{0:T(512)S(1)}, f32[512]{0:T(512)}, u32[]{:S(2)}) copy-start(f32[512]{0:T(512)} %param.20) | copy-start | bytes 6148
  95.5 0.7 copy-start.7
  111.0 0.7 copy-start.3
  111.0 0.7 copy-start.5
  111.0 0.7 copy-start.4
  111.0 0.7 copy-start.6
Sparse Core Ops, SparseCore 0:
  111.1 265.9 all-reduce.3
where the time goes:
time: 389 us
  waiting for transfers between devices  189 us (49%)
  blocking collectives  141 us (36%)
  matrix products  22.6 us (6%)
  between operations  14.4 us (4%)
  other arithmetic  11.6 us (3%)
  local copies, waits for them, and re-layouts  10.3 us (3%)
    psum x1, waiting for transfers between devices, local(): first, hidden, last = lax.psum((first, hidden, last), BOTH)  189 us
    psum x1, blocking collectives, local(): first, hidden, last = lax.psum((first, hidden, last), BOTH)  73.2 us
    all_gather x1, blocking collectives, local(): everyone = lax.all_gather(mine, BOTH)  67.6 us
    dot_general x8, matrix products, forward(): jnp.dot(jnp.concatenate([hidden, tangent], 0), w_hidden[level], precision...  9.35 us
  transfers between devices with their start and end apart: 1, of which 1 were waited for; matrix products, arithmetic and copies ran while one was open for 1% of the time, Pallas kernels for 0%

commit v1 on v0

--- a/solution.py
+++ b/solution.py
@@ -112,7 +112,9 @@
         w_first,
         w_hidden,
     )
-    first, hidden, last = lax.psum((first, hidden, last), BOTH)
+    first, hidden, last = lax.psum(
+        lax.psum((first, hidden, last), axis_name="wide"), axis_name="narrow"
+    )
     return (integral, first, hidden, last)
 
 

time: 389 us -> 458 us (1.18)
  blocking collectives: 141 us -> 206 us
    psum x1 -> x2, blocking collectives: 73.2 us -> 139 us  [the longest x1 130 us: local(): lax.psum((first, hidden, last), axis_name='wide')]
    psum x1 -> x2, waiting for transfers between devices: 189 us -> 192 us  [the longest x1 192 us: local(): lax.psum((first, hidden, last), axis_name='wide')]
  transfers between devices with their start and end apart: 1 -> 2, of which waited for: 1 -> 1; matrix products, arithmetic and copies ran while one was open for 1% -> 1% of each run, Pallas kernels for 0% -> 0%
where the time goes in v1:
time: 458 us; the launch traced here: 457 us
  blocking collectives  206 us (45%)
  waiting for transfers between devices  192 us (42%)
  matrix products  22.6 us (5%)
  between operations  14.4 us (3%)
  other arithmetic  11.6 us (3%)
  local copies, waits for them, and re-layouts  10.3 us (2%)
    psum x1, waiting for transfers between devices, local(): lax.psum((first, hidden, last), axis_name='wide')  192 us
    psum x1, blocking collectives, local(): lax.psum((first, hidden, last), axis_name='wide')  130 us
    all_gather x1, blocking collectives, local(): everyone = lax.all_gather(mine, BOTH)  67.6 us
    dot_general x8, matrix products, forward(): jnp.dot(jnp.concatenate([hidden, tangent], 0), w_hidden[level], precision...  9.35 us
    psum x1, blocking collectives, local(): lax.psum(lax.psum((first, hidden, last), axis_name='wide'), axis_name='na...  9.27 us
  transfers between devices with their start and end apart: 2, of which 1 were waited for; matrix products, arithmetic and copies ran while one was open for 1% of the time, Pallas kernels for 0%

profile of v1, /device:TPU:2, one launch (start us, length us, event | category | flops | bytes accessed | tf_op | source)
XLA Modules:
  0.0 457.4 jit_solution(1836947949143250377)
XLA Ops:
  7.2 0.0 all-reduce.6.cloned.1.call-start
  7.2 0.8 fusion.155
  8.0 0.8 fusion.156
  8.7 0.8 fusion.154
  9.5 0.9 fusion.153
  10.4 0.8 slice_bitcast_fusion.1
  11.2 0.8 add_tanh_fusion.1
  12.0 1.8 fusion.78
  13.9 0.0 copy-start
  13.9 0.1 subtract_multiply_fusion.7
  13.9 2.0 fusion.74
  16.0 0.1 subtract_multiply_fusion.6
  16.0 0.3 copy-done
  16.4 0.7 fusion.70
  17.0 0.0 copy-start.8
  17.0 0.0 copy-start.9
  17.0 0.0 copy-start.1
  17.1 0.1 subtract_multiply_fusion.5
  17.1 0.6 fusion.66
  17.8 0.0 copy-done.8
  17.8 0.0 copy-done.9
  17.8 0.0 copy-start.2
  17.8 0.0 copy-done.1
  17.8 0.2 multiply_reduce_fusion.2
  18.0 67.6 %all-gather.1 = f32[256,2,128]{2,1,0:T(2,128)S(1)} all-gather(f32[1,2,128]{2,1,0:T(2,128)S(1)} %maximum_bitcast_fusion), channel_id=2, replica_groups=mesh['wide'=64,'narrow'=4] {'wide','narrow'}, dimensions={0}, use_global_device_ids=true | all-gather | bytes 263168 | tf_op jit(solution)/shard_map/all_gather | solution.py:83
  85.6 0.2 fusion.152
  85.8 4.7 %select_reduce_fusion = (f32[128]{0:T(128)S(1)}, f32[128]{0:T(128)}) fusion(f32[32768]{0:T(1024)S(1)} %bitcast.67, f32[32768]{0:T(1024)S(1)} %bitcast.66, f32[128]{0:T(128)S(1)} %get-tuple-element.76, f32[128]{0:T(128)S(1)} %get-tuple-element.77), kind=kLoop, calls=%fused_computation | loop fusion | flops 25165568 | bytes 264192 | tf_op jit(solution)/shard_map/reduce_sum | solution.py:88
  90.5 0.0 copy-done.2
  90.5 0.3 add_tanh_fusion
  90.8 1.0 fusion.48
  91.8 0.2 subtract_multiply_fusion.3
  92.0 1.1 fusion.52
  93.1 0.2 subtract_multiply_fusion.2
  93.2 1.1 fusion.56
  94.3 0.2 subtract_multiply_fusion.1
  94.5 1.0 fusion.60
  95.5 0.0 copy-start.7
  95.5 0.2 multiply_reduce_fusion
  95.8 0.4 copy-done.7
  96.2 0.4 fusion.102
  96.7 1.5 fusion.32
  98.2 1.7 fusion.47
  99.9 0.4 fusion.97
  100.3 1.5 fusion.35
  101.8 1.5 fusion.46
  103.3 0.4 fusion.96
  103.7 1.5 fusion.38
  105.2 1.5 fusion.45
  106.6 0.4 fusion.95
  107.0 1.5 fusion.41
  108.5 2.5 pad_maximum_fusion
  111.0 0.0 all-reduce.6.cloned.1.call-update
  111.0 0.0 all-reduce.8.cloned.1.call-start
  111.1 191.9 %all-reduce.6.cloned.1.call-done = f32[4,512,512]{2,1,0:T(8,128)} async-done(((f32[4,512,512]{2,1,0:T(8,128)}), f32[4,512,512]{2,1,0:T(8,128)}) %all-reduce.6.cloned.1.call-update) | async-done | bytes 4194320 | tf_op jit(solution)/shard_map/psum | solution.py:116
  303.0 0.0 all-reduce.8.cloned.1.call-update
  303.0 0.6 copy-done.3
  303.7 0.0 copy-done.5
  303.7 0.0 copy-done.4
  303.7 0.0 copy-done.6
  303.7 2.7 fusion.44
  306.4 0.6 add_reduce_fusion.1
  307.0 129.6 %all-reduce.1 = (f32[2,512]{1,0:T(2,128)S(1)}, f32[512]{0:T(512)S(1)}) all-reduce(f32[2,512]{1,0:T(2,128)S(1)} %pad_maximum_fusion.18, f32[512]{0:T(512)S(1)} %get-tuple-element.45), channel_id=1, replica_groups=mesh['wide'=64,'narrow'=4] {'wide'}, use_global_device_ids=true, to_apply=%region_7.8 | all-reduce | flops 1536 | bytes 12288 | tf_op jit(solution)/shard_map/psum | solution.py:116
  436.7 9.3 %all-reduce.2 = (f32[2,512]{1,0:T(2,128)}, f32[512]{0:T(512)}) all-reduce(f32[2,512]{1,0:T(2,128)S(1)} %get-tuple-element.14, f32[512]{0:T(512)S(1)} %get-tuple-element.15), channel_id=1, replica_groups=mesh['wide'=64,'narrow'=4] {'narrow'}, use_global_device_ids=true, to_apply=%region_8.9 | all-reduce | flops 1536 | bytes 12288 | tf_op jit(solution)/shard_map/psum | solution.py:115
  445.9 4.6 %copy.20 = f32[4,512,512]{2,1,0:T(8,128)} copy(f32[4,512,512]{2,1,0:T(8,128)} %all-reduce.8.cloned.1.call-done) | data formatting | bytes 8388608
  (16 shorter events, 0.1 us)
Async XLA Ops:
  7.2 295.8 %all-reduce.6.cloned.1.call-start = ((), (), s32[]{:S(2)}) async-start(), calls=%async_computation | async-start | bytes 8388608 | tf_op jit(solution)/shard_map/psum | solution.py:116
  13.9 2.5 copy-start
  17.0 0.8 copy-start.8
  17.0 0.8 copy-start.9
  17.0 0.8 copy-start.1
  17.8 72.7 %copy-start.2 = (f32[512]{0:T(512)S(1)}, f32[512]{0:T(512)}, u32[]{:S(2)}) copy-start(f32[512]{0:T(512)} %param.20) | copy-start | bytes 6148
  95.5 0.7 copy-start.7
  111.0 334.9 %all-reduce.8.cloned.1.call-start = ((), (), s32[]{:S(2)}) async-start(), calls=%async_computation.1 | async-start | bytes 8388608 | tf_op jit(solution)/shard_map/psum | solution.py:115
  303.0 0.7 copy-start.3
  303.0 0.7 copy-start.5
  303.0 0.7 copy-start.4
  303.0 0.7 copy-start.6
Sparse Core Ops, SparseCore 0:
  111.1 191.8 all-reduce.5
  305.3 95.5 all-reduce.7
